TPU v7x, 32 devices: a whole 2x2x4 slice. The times are simulated.
32 devices in a mesh: leaf: 2 (over core), row: 4 (over y, x), col: 4 (over z).
Axes of the slice: x: 2, y: 2, z: 4, core: 2. Of those that a mesh axis runs over, the one named last changes fastest.
Arguments:
- rhs_leaf: bfloat16 [2, 8, 64, 2048], P('leaf', None, None, 'col'), may hold values from -6 to 6
- dinv_leaf: bfloat16 [2, 8, 2048, 2048], P('leaf', None, 'row', 'col'), as said below
- panel_leaf: bfloat16 [2, 8, 1024, 2048], P('leaf', None, 'col', 'row'), may hold values from -0.0625 to 0.0625
- counts: int32 [2, 8], P('leaf'), may hold values from 256 to 2048, as said below
- row_index: int32 [2, 8, 1024], P('leaf'), may hold values from 0 to 4095, as said below
- rhs_root: bfloat16 [64, 4096], P(None, 'col'), may hold values from -6 to 6
- dinv_root: bfloat16 [4096, 4096], P(('leaf', 'row')), as said below
Outputs:
- y_leaf: bfloat16 [2, 8, 64, 2048], P('leaf', None, None, 'row')
- y_root: bfloat16 [64, 4096], P(None, ('leaf', 'row'))
Inputs may be any that keep to these rules, and one draw needn't show every extreme that they name: `counts`: each subtree supernode has at least 256 columns; at least one supernode of every draw has all 2048. `row_index`: within one supernode the 1024 entries are distinct and increasing. `dinv_leaf`: each [2048, 2048] block is lower triangular with a nonzero diagonal. `dinv_root`: lower triangular with a nonzero diagonal.
All inputs are finite; a program needn't handle non-finite values.
Results may differ from a plain program's by a relative error of at most 0.0053.
Values may be sent and summed in bfloat16 or wider, within the bound.
No kernel may reach another device: no remote copies, remote signals or barrier semaphores. Data moves between devices by JAX's collectives and lax.ppermute only.
A program may use at most 64 MiB of HBM per device.

v0:
```python
import jax
import jax.numpy as jnp
from jax import lax
from jax.sharding import PartitionSpec as P


def local(rhs_leaf, dinv_leaf, panel_leaf, counts, row_index, rhs_root, dinv_root):
    width_col = rhs_leaf.shape[3]
    width_row = dinv_leaf.shape[2]
    panel_rows = panel_leaf.shape[2]
    columns = rhs_root.shape[0]
    sep_width = rhs_root.shape[1] * lax.axis_size("col")
    limit = counts[0][:, None, None]
    col_slots = lax.axis_index("col") * width_col + lax.iota(jnp.int32, width_col)
    masked = jnp.where(col_slots[None, None, :] < limit, rhs_leaf[0], jnp.zeros((), jnp.bfloat16))
    partial_value = jnp.einsum(
        "kbj,kij->kbi", masked, dinv_leaf[0], preferred_element_type=jnp.float32
    )
    summed = lax.psum(partial_value, "col")
    row_slots = lax.axis_index("row") * width_row + lax.iota(jnp.int32, width_row)
    live_rows = (row_slots[None, None, :] < limit).astype(jnp.float32)
    solved = (summed * live_rows).astype(jnp.bfloat16)
    update = jnp.einsum("kbi,kri->kbr", solved, panel_leaf[0], preferred_element_type=jnp.float32)
    offset = lax.axis_index("col") * panel_rows
    targets = lax.dynamic_slice_in_dim(row_index[0], offset, panel_rows, 1)
    flat_update = jnp.transpose(update, (1, 0, 2)).reshape(columns, -1)
    accum = jnp.zeros((columns, sep_width), jnp.float32).at[:, targets.reshape(-1)].add(flat_update)
    piece = lax.psum_scatter(accum, "col", scatter_dimension=1, tiled=True)
    share = lax.psum(piece, ("leaf", "row"))
    reduced = (rhs_root.astype(jnp.float32) - share).astype(jnp.bfloat16)
    whole_reduced = lax.all_gather(reduced, "col", axis=1, tiled=True)
    y_root = jnp.dot(whole_reduced, dinv_root.T, preferred_element_type=jnp.float32).astype(
        jnp.bfloat16
    )
    return (solved[None], y_root)


def solution(mesh):
    in_specs = (
        P("leaf", None, None, "col"),
        P("leaf", None, "row", "col"),
        P("leaf", None, "col", "row"),
        P("leaf", None),
        P("leaf", None, None),
        P(None, "col"),
        P(("leaf", "row"), None),
    )
    out_specs = (P("leaf", None, None, "row"), P(None, ("leaf", "row")))
    return jax.shard_map(local, mesh=mesh, in_specs=in_specs, out_specs=out_specs, check_vma=False)
```

profile of v0, /device:TPU:0, one launch (start us, length us, event | category | flops | bytes accessed | tf_op | source)
XLA Modules:
  0.0 218.8 jit_solution(5079778243573968000)
XLA Ops:
  7.2 0.0 copy-start
  7.2 0.0 all-reduce.3.cloned.1.call-start
  7.2 0.9 compare_convert_fusion
  8.1 4.7 %fusion = f32[8,64,512]{2,1,0:T(8,128)} fusion(bf16[1,8,512,512]{3,2,1,0:T(8,128)(2,1)} %param.8, bf16[1,8,64,512]{3,2,1,0:T(8,128)(2,1)} %param.7, pred[8,512]{1,0:T(8,128)(4,1)S(1)} %get-tuple-element.3), kind=kOutput, calls=%fused_computation.1 | convolution fusion | flops 268697600 | bytes 5771264 | tf_op jit(solution)/shard_map/kbj,kij->kbi/dot_general | solution.py:16
  12.8 0.0 all-reduce.3.cloned.1.call-update
  12.8 0.0 reduce-scatter.2.cloned.1.call-start
  12.9 0.7 dynamic-slice_bitcast_fusion
  13.6 54.0 %all-reduce.3.cloned.1.call-done = f32[8,64,512]{2,1,0:T(8,128)} async-done(((f32[8,64,512]{2,1,0:T(8,128)}), f32[8,64,512]{2,1,0:T(8,128)}) %all-reduce.3.cloned.1.call-update) | async-done | bytes 1048592 | tf_op jit(solution)/shard_map/psum | solution.py:19
  67.6 0.0 copy-done
  67.6 2.0 fusion.4
  69.6 0.1 copy.13
  69.7 1.3 copy.12
  71.0 0.0 copy-start.2
  71.0 0.0 copy-start.1
  71.0 13.3 %scatter_custom_fusion = f32[64,4096]{0,1:T(8,128)} fusion(s32[2048]{0:T(1024)S(1)} %bitcast.29, f32[2048,64]{1,0:T(8,128)} %copy.12, f32[]{:T(128)} %constant.7.clone.1), kind=kCustom, calls=%fused_computation.7 | custom fusion | flops 131072 | bytes 1049088 | tf_op jit(solution)/shard_map/scatter-add | solution.py:27
  84.3 0.0 reduce-scatter.2.cloned.1.call-update
  84.3 0.0 all-reduce.5.cloned.1.call-start
  84.4 0.0 copy-done.2
  84.4 0.2 copy.10
  84.6 42.8 %reduce-scatter.2.cloned.1.call-done = f32[64,1024]{0,1:T(8,128)} async-done(((f32[64,4096]{0,1:T(8,128)}), f32[64,1024]{0,1:T(8,128)}) %reduce-scatter.2.cloned.1.call-update) | async-done | bytes 262160 | tf_op jit(solution)/shard_map/reduce_scatter | solution.py:28
  127.4 0.0 all-reduce.5.cloned.1.call-update
  127.4 0.0 copy-done.1
  127.4 0.9 fusion.11
  128.4 56.2 %all-reduce.5.cloned.1.call-done = f32[64,1024]{0,1:T(8,128)} async-done(((f32[64,1024]{0,1:T(8,128)}), f32[64,1024]{0,1:T(8,128)}) %all-reduce.5.cloned.1.call-update) | async-done | bytes 262160 | tf_op jit(solution)/shard_map/psum | solution.py:29
  184.5 1.1 subtract_convert_fusion
  185.6 22.4 %all_gather.3 = bf16[64,4096]{0,1:T(8,128)(2,1)S(1)} all-gather(bf16[64,1024]{0,1:T(8,128)(2,1)S(1)} %subtract_convert_fusion), channel_id=1, replica_groups=mesh['leaf'=2,'row'=4,'col'=4] {'col'}, dimensions={1}, use_global_device_ids=true | all-gather | bytes 655360 | tf_op jit(solution)/shard_map/all_gather | solution.py:31
  208.0 4.2 %convolution_convert_fusion = bf16[64,512]{1,0:T(8,128)(2,1)} fusion(bf16[64,4096]{0,1:T(8,128)(2,1)S(1)} %all_gather.3, bf16[512,4096]{1,0:T(8,128)(2,1)} %param.13), kind=kOutput, calls=%fused_computation.6 | convolution fusion | flops 268468224 | bytes 4784128 | tf_op jit(solution)/shard_map/dot_general | solution.py:32
  (3 shorter events, 0.0 us)
Async XLA Ops:
  7.2 60.5 %copy-start = (bf16[1,8,256,512]{3,2,1,0:T(8,128)(2,1)S(1)}, bf16[1,8,256,512]{3,2,1,0:T(8,128)(2,1)}, u32[]{:S(2)}) copy-start(bf16[1,8,256,512]{3,2,1,0:T(8,128)(2,1)} %param.9) | copy-start | bytes 6291460
  7.2 60.4 %all-reduce.3.cloned.1.call-start = ((), (), s32[]{:S(2)}) async-start(), calls=%async_computation.1 | async-start | bytes 2097152 | tf_op jit(solution)/shard_map/psum | solution.py:19
  12.8 114.6 %reduce-scatter.2.cloned.1.call-start = ((), (), s32[]{:S(2)}) async-start(), calls=%async_computation.2 | async-start | bytes 2621440 | tf_op jit(solution)/shard_map/reduce_scatter | solution.py:28
  71.0 13.4 %copy-start.2 = (bf16[64,1024]{1,0:T(8,128)(2,1)S(1)}, bf16[64,1024]{1,0:T(8,128)(2,1)}, u32[]{:S(2)}) copy-start(bf16[64,1024]{1,0:T(8,128)(2,1)} %param.12) | copy-start | bytes 393220
  71.0 56.5 %copy-start.1 = (f32[8,64,512]{2,1,0:T(8,128)S(1)}, f32[8,64,512]{2,1,0:T(8,128)}, u32[]{:S(2)}) copy-start(f32[8,64,512]{2,1,0:T(8,128)} %all-reduce.3.cloned.1.call-done) | copy-start | bytes 3145732
  84.3 100.2 %all-reduce.5.cloned.1.call-start = ((), (), s32[]{:S(2)}) async-start(), calls=%async_computation.3 | async-start | bytes 1048576 | tf_op jit(solution)/shard_map/psum | solution.py:29
Sparse Core Ops, SparseCore 0:
  13.0 54.6 all-reduce.2
  84.5 42.8 reduce-scatter.1
  130.5 53.9 all-reduce.4
where the time goes:
time: 219 us
  waiting for transfers between devices  153 us (70%)
  blocking collectives  22.4 us (10%)
  other arithmetic  16.2 us (7%)
  between operations  13.8 us (6%)
  matrix products  10.9 us (5%)
  local copies, waits for them, and re-layouts  2.27 us (1%)
    psum x1, waiting for transfers between devices, local(): share = lax.psum(piece, ('leaf', 'row'))  56.2 us
    psum x1, waiting for transfers between devices, local(): summed = lax.psum(partial_value, 'col')  54 us
    reduce_scatter x1, waiting for transfers between devices, local(): piece = lax.psum_scatter(accum, 'col', scatter_dimension=1, tiled=True)  42.8 us
    all_gather x1, blocking collectives, local(): whole_reduced = lax.all_gather(reduced, 'col', axis=1, tiled=True)  22.4 us
    scatter-add x1, other arithmetic, local(): jnp.zeros((columns, sep_width), jnp.float32).at[:, targets.reshape(-1)]  13.3 us
    dot_general x1, matrix products, local(): jnp.einsum('kbj,kij->kbi', masked, dinv_leaf[0], preferred_element_type=j...  4.71 us
  transfers between devices with their start and end apart: 3, of which 3 were waited for; matrix products, arithmetic and copies ran while one was open for 1% of the time, Pallas kernels for 0%

commit v1 on v0

--- a/solution.py
+++ b/solution.py
@@ -26,7 +26,10 @@
     flat_update = jnp.transpose(update, (1, 0, 2)).reshape(columns, -1)
     accum = jnp.zeros((columns, sep_width), jnp.float32).at[:, targets.reshape(-1)].add(flat_update)
     piece = lax.psum_scatter(accum, "col", scatter_dimension=1, tiled=True)
-    share = lax.psum(piece, ("leaf", "row"))
+    point_fill = lambda buf, a_name, mesh_ax: lax.psum(
+        lax.psum(buf, axis_name=a_name), axis_name=mesh_ax
+    )
+    share = point_fill(piece, "row", "leaf")
     reduced = (rhs_root.astype(jnp.float32) - share).astype(jnp.bfloat16)
     whole_reduced = lax.all_gather(reduced, "col", axis=1, tiled=True)
     y_root = jnp.dot(whole_reduced, dinv_root.T, preferred_element_type=jnp.float32).astype(

time: 219 us -> 231 us (1.055)
  waiting for transfers between devices: 153 us -> 164 us
    psum x1 -> x2, waiting for transfers between devices: 56.2 us -> 67.2 us  [the longest x1 47.3 us: local(): lax.psum(buf, axis_name=a_name)]
  transfers between devices with their start and end apart: 3 -> 4, of which waited for: 3 -> 4; matrix products, arithmetic and copies ran while one was open for 1% -> 1% of each run, Pallas kernels for 0% -> 0%
where the time goes in v1:
time: 231 us; the launch traced here: 230 us
  waiting for transfers between devices  164 us (71%)
  blocking collectives  22.9 us (10%)
  other arithmetic  16.1 us (7%)
  between operations  13.8 us (6%)
  matrix products  10.9 us (5%)
    psum x1, waiting for transfers between devices, local(): summed = lax.psum(partial_value, 'col')  54 us
    psum x1, waiting for transfers between devices, local(): lax.psum(buf, axis_name=a_name)  47.3 us
    reduce_scatter x1, waiting for transfers between devices, local(): piece = lax.psum_scatter(accum, 'col', scatter_dimension=1, tiled=True)  43 us
    all_gather x1, blocking collectives, local(): whole_reduced = lax.all_gather(reduced, 'col', axis=1, tiled=True)  22.9 us
    psum x1, waiting for transfers between devices, local(): lax.psum(lax.psum(buf, axis_name=a_name), axis_name=mesh_ax)  19.9 us
    scatter-add x1, other arithmetic, local(): jnp.zeros((columns, sep_width), jnp.float32).at[:, targets.reshape(-1)]  13.2 us
    dot_general x1, matrix products, local(): jnp.einsum('kbj,kij->kbi', masked, dinv_leaf[0], preferred_element_type=j...  4.71 us
  transfers between devices with their start and end apart: 4, of which 4 were waited for; matrix products, arithmetic and copies ran while one was open for 1% of the time, Pallas kernels for 0%

profile of v1, /device:TPU:0, one launch (start us, length us, event | category | flops | bytes accessed | tf_op | source)
XLA Modules:
  0.0 230.4 jit_solution(4059251930167812860)
XLA Ops:
  7.2 0.0 copy-start
  7.2 0.0 all-reduce.4.cloned.1.call-start
  7.2 0.9 compare_convert_fusion
  8.1 4.7 %fusion = f32[8,64,512]{2,1,0:T(8,128)} fusion(bf16[1,8,512,512]{3,2,1,0:T(8,128)(2,1)} %param.8, bf16[1,8,64,512]{3,2,1,0:T(8,128)(2,1)} %param.7, pred[8,512]{1,0:T(8,128)(4,1)S(1)} %get-tuple-element.3), kind=kOutput, calls=%fused_computation.1 | convolution fusion | flops 268697600 | bytes 5771264 | tf_op jit(solution)/shard_map/kbj,kij->kbi/dot_general | solution.py:16
  12.8 0.0 all-reduce.4.cloned.1.call-update
  12.8 0.0 reduce-scatter.2.cloned.1.call-start
  12.9 0.7 dynamic-slice_bitcast_fusion
  13.6 54.0 %all-reduce.4.cloned.1.call-done = f32[8,64,512]{2,1,0:T(8,128)} async-done(((f32[8,64,512]{2,1,0:T(8,128)}), f32[8,64,512]{2,1,0:T(8,128)}) %all-reduce.4.cloned.1.call-update) | async-done | bytes 1048592 | tf_op jit(solution)/shard_map/psum | solution.py:19
  67.6 0.0 copy-done
  67.6 2.0 fusion.4
  69.6 0.1 copy.13
  69.7 1.3 copy.12
  71.0 0.0 copy-start.2
  71.0 13.2 %scatter_custom_fusion = f32[64,4096]{0,1:T(8,128)} fusion(s32[2048]{0:T(1024)S(1)} %bitcast.29, f32[2048,64]{1,0:T(8,128)} %copy.12, f32[]{:T(128)} %constant.7.clone.1), kind=kCustom, calls=%fused_computation.7 | custom fusion | flops 131072 | bytes 1049088 | tf_op jit(solution)/shard_map/scatter-add | solution.py:27
  84.2 0.0 copy-start.1
  84.2 0.0 reduce-scatter.2.cloned.1.call-update
  84.2 0.0 all-reduce.6.cloned.1.call-start
  84.3 43.0 %reduce-scatter.2.cloned.1.call-done = f32[64,1024]{0,1:T(8,128)} async-done(((f32[64,4096]{0,1:T(8,128)}), f32[64,1024]{0,1:T(8,128)}) %reduce-scatter.2.cloned.1.call-update) | async-done | bytes 262160 | tf_op jit(solution)/shard_map/reduce_scatter | solution.py:28
  127.3 0.0 all-reduce.6.cloned.1.call-update
  127.3 0.0 all-reduce.8.cloned.1.call-start
  127.4 0.0 copy-done.2
  127.4 0.2 copy.10
  127.6 47.3 %all-reduce.6.cloned.1.call-done = f32[64,1024]{0,1:T(8,128)} async-done(((f32[64,1024]{0,1:T(8,128)}), f32[64,1024]{0,1:T(8,128)}) %all-reduce.6.cloned.1.call-update) | async-done | bytes 262160 | tf_op jit(solution)/shard_map/psum | solution.py:30
  174.9 0.0 all-reduce.8.cloned.1.call-update
  174.9 0.0 copy-done.1
  174.9 0.9 fusion.11
  175.8 19.9 %all-reduce.8.cloned.1.call-done = f32[64,1024]{0,1:T(8,128)} async-done(((f32[64,1024]{0,1:T(8,128)}), f32[64,1024]{0,1:T(8,128)}) %all-reduce.8.cloned.1.call-update) | async-done | bytes 262160 | tf_op jit(solution)/shard_map/psum | solution.py:29
  195.7 1.1 subtract_convert_fusion
  196.8 22.9 %all_gather.3 = bf16[64,4096]{0,1:T(8,128)(2,1)S(1)} all-gather(bf16[64,1024]{0,1:T(8,128)(2,1)S(1)} %subtract_convert_fusion), channel_id=1, replica_groups=mesh['leaf'=2,'row'=4,'col'=4] {'col'}, dimensions={1}, use_global_device_ids=true | all-gather | bytes 655360 | tf_op jit(solution)/shard_map/all_gather | solution.py:34
  219.7 4.2 %convolution_convert_fusion = bf16[64,512]{1,0:T(8,128)(2,1)} fusion(bf16[64,4096]{0,1:T(8,128)(2,1)S(1)} %all_gather.3, bf16[512,4096]{1,0:T(8,128)(2,1)} %param.13), kind=kOutput, calls=%fused_computation.6 | convolution fusion | flops 268468224 | bytes 4784128 | tf_op jit(solution)/shard_map/dot_general | solution.py:35
  (3 shorter events, 0.0 us)
Async XLA Ops:
  7.2 60.5 %copy-start = (bf16[1,8,256,512]{3,2,1,0:T(8,128)(2,1)S(1)}, bf16[1,8,256,512]{3,2,1,0:T(8,128)(2,1)}, u32[]{:S(2)}) copy-start(bf16[1,8,256,512]{3,2,1,0:T(8,128)(2,1)} %param.9) | copy-start | bytes 6291460
  7.2 60.4 %all-reduce.4.cloned.1.call-start = ((), (), s32[]{:S(2)}) async-start(), calls=%async_computation.1 | async-start | bytes 2097152 | tf_op jit(solution)/shard_map/psum | solution.py:19
  12.8 114.5 %reduce-scatter.2.cloned.1.call-start = ((), (), s32[]{:S(2)}) async-start(), calls=%async_computation.2 | async-start | bytes 2621440 | tf_op jit(solution)/shard_map/reduce_scatter | solution.py:28
  71.0 56.4 %copy-start.2 = (bf16[64,1024]{1,0:T(8,128)(2,1)S(1)}, bf16[64,1024]{1,0:T(8,128)(2,1)}, u32[]{:S(2)}) copy-start(bf16[64,1024]{1,0:T(8,128)(2,1)} %param.12) | copy-start | bytes 393220
  84.2 90.7 %copy-start.1 = (f32[8,64,512]{2,1,0:T(8,128)S(1)}, f32[8,64,512]{2,1,0:T(8,128)}, u32[]{:S(2)}) copy-start(f32[8,64,512]{2,1,0:T(8,128)} %all-reduce.4.cloned.1.call-done) | copy-start | bytes 3145732
  84.2 90.6 %all-reduce.6.cloned.1.call-start = ((), (), s32[]{:S(2)}) async-start(), calls=%async_computation.3 | async-start | bytes 1048576 | tf_op jit(solution)/shard_map/psum | solution.py:30
  127.3 68.4 %all-reduce.8.cloned.1.call-start = ((), (), s32[]{:S(2)}) async-start(), calls=%async_computation.4 | async-start | bytes 1048576 | tf_op jit(solution)/shard_map/psum | solution.py:29
Sparse Core Ops, SparseCore 0:
  13.0 54.6 all-reduce.3
  84.4 42.8 reduce-scatter.1
  130.3 44.5 all-reduce.5
  177.1 18.5 all-reduce.7
